TPU v7x, 32 devices: a whole 2x2x4 slice. The times are simulated.
32 devices in a mesh: cls: 32 (over z, y, x, core).
Axes of the slice: x: 2, y: 2, z: 4, core: 2. Of those that a mesh axis runs over, the one named last changes fastest.
Arguments:
- features: bfloat16 [512, 12544], P('cls'), may hold values from -6 to 6
- fc_weight: bfloat16 [12544, 512], replicated, may hold values from -0.0546875 to 0.0546875
- centers: bfloat16 [131072, 512], P('cls'), may hold values from -6 to 6
- labels: int32 [512], replicated, may hold values from 0 to 131071
Outputs:
- loss: float32 [512], P('cls')
- grad_centers: bfloat16 [131072, 512], P('cls')
- grad_fc: float32 [12544, 512], P('cls')
All inputs are finite; a program needn't handle non-finite values.
Results may differ from a plain program's by a relative error of at most 0.0078.
Values may be sent and summed in bfloat16 or wider, within the bound.
A program may use at most 128 MiB of HBM per device.

v0:
```python
import functools
import math

import jax
import jax.numpy as jnp
from jax import lax
from jax.experimental import pallas as pl
from jax.experimental.pallas import tpu as pltpu
from jax.sharding import PartitionSpec as P

logit_scale = 64.0
cos_margin = math.cos(0.5)
sin_margin = math.sin(0.5)
epsilon = 1e-06
MESH = pl.DeviceIdType.MESH
f32, bf16 = jnp.float32, jnp.bfloat16


def inverse_norm(values):
    return lax.rsqrt(jnp.sum(values * values, axis=1, keepdims=True) + epsilon)


def largest_divisor(number, most):
    return next(d for d in range(most, 0, -1) if number % d == 0)


def kernel(
    n, rows, slots, feat, weight, centers_hbm, labels,
    loss_out, gc_out, fc_out,
    wbuf, cbuf, clow, inv_c, cosines, acc, esend, emb, fsend, frecv,
    ssend, srecv, psend, pair, precv, gsend, grecv, stage,
    wsem, csem, osem, ssems, rsems,
):
    me = lax.axis_index("cls")
    tok, feats = feat.shape
    classes, width = cbuf.shape
    batch = n * tok
    chunk = wbuf.shape[1]
    chunks = feats // chunk
    blocks = classes // rows
    part = feats // n
    half = n // 2
    core = lax.rem(me, 2)
    chip = me // 2
    partner = me + 1 - 2 * core

    def weight_copy(c):
        return pltpu.make_async_copy(
            weight.at[pl.ds(c * chunk, chunk)], wbuf.at[c % slots], wsem.at[c % slots]
        )

    for c in range(min(slots, chunks)):
        weight_copy(c).start()
    centers_copy = pltpu.make_async_copy(centers_hbm, cbuf, csem)
    centers_copy.start()

    barrier = pltpu.get_barrier_semaphore()

    def greet(i, carry):
        pl.semaphore_signal(barrier, inc=1, device_id=(lax.rem(me + i, n),), device_id_type=MESH)
        return carry

    lax.fori_loop(1, n, greet, 0)

    for j in range(n):
        fsend[j] = feat[:, j * part : (j + 1) * part]

    total = jnp.zeros((tok, width), f32)
    for c in range(chunks):
        weight_copy(c).wait()
        total = total + jnp.dot(
            feat[:, c * chunk : (c + 1) * chunk], wbuf[c % slots], preferred_element_type=f32
        )
        if c + slots < chunks:
            weight_copy(c + slots).start()
    esend[...] = total.astype(bf16)
    emb[me] = total.astype(bf16)
    pl.semaphore_wait(barrier, n - 1)

    def send_to(phase, source, target, first, last):
        def step(i, carry):
            dst = lax.rem(me + i, n)
            pltpu.make_async_remote_copy(
                src_ref=source(dst), dst_ref=target.at[me],
                send_sem=ssems.at[phase], recv_sem=rsems.at[phase],
                device_id=(dst,), device_id_type=MESH,
            ).start()
            return carry

        lax.fori_loop(first, last, step, 0)

    def wait_all(sems, phase, target, count):
        whole = target.at[pl.ds(0, count)]
        pltpu.make_async_copy(whole, whole, sems.at[phase]).wait()

    def send_chips(phase, source, target, slot):
        def step(i, carry):
            to = lax.rem(chip + i, half)
            pltpu.make_async_remote_copy(
                src_ref=source(to), dst_ref=target.at[slot],
                send_sem=ssems.at[phase], recv_sem=rsems.at[phase],
                device_id=(2 * to + core,), device_id_type=MESH,
            ).start()
            return carry

        lax.fori_loop(1, half, step, 0)

    def send_partner(phase, source, target):
        def step(j, carry):
            pltpu.make_async_remote_copy(
                src_ref=source(j), dst_ref=target(j),
                send_sem=ssems.at[phase], recv_sem=rsems.at[phase],
                device_id=(partner,), device_id_type=MESH,
            ).start()
            return carry

        lax.fori_loop(0, half, step, 0)

    send_chips(0, lambda to: esend, emb, me)

    centers_copy.wait()

    def normalise(k, carry):
        at = pl.ds(pl.multiple_of(k * rows, rows), rows)
        block = cbuf[at].astype(f32)
        inv = inverse_norm(block)
        inv_c[at] = inv
        clow[at] = (block * inv).astype(bf16)
        return carry

    lax.fori_loop(0, blocks, normalise, 0)

    wait_all(rsems, 0, emb, half - 1)
    send_partner(5, lambda j: emb.at[2 * j + core], lambda j: emb.at[2 * j + core])
    send_to(1, lambda dst: fsend.at[dst], frecv, 1, half)
    frecv[me] = fsend[me]
    wait_all(rsems, 5, emb, half)
    wait_all(ssems, 5, emb, half)

    all_emb = emb[...].reshape(batch, width).astype(f32)
    emb_low = (all_emb * inverse_norm(all_emb)).astype(bf16)
    emb[...] = emb_low.reshape(n, tok, width)

    local = labels[...] - me * classes
    class_ids = lax.broadcasted_iota(jnp.int32, (rows, batch), 0)

    def forward(k, carry):
        esum, tcos = carry
        at = pl.ds(pl.multiple_of(k * rows, rows), rows)
        cos = lax.dot_general(
            clow[at], emb[...].reshape(batch, width), (((1,), (1,)), ((), ())),
            preferred_element_type=f32,
        )
        cosines[at] = cos
        hit = class_ids == local - k * rows
        tcos = tcos + jnp.sum(jnp.where(hit, cos, 0.0), axis=0, keepdims=True)
        powers = jnp.exp(logit_scale * cos - logit_scale)
        esum = esum + jnp.sum(jnp.where(hit, 0.0, powers), axis=0, keepdims=True)
        return esum, tcos

    zero_row = jnp.zeros((1, batch), f32)
    esum, tcos = lax.fori_loop(0, blocks, forward, (zero_row, zero_row))
    mine = (local >= 0) & (local < classes)
    tsin = jnp.sqrt(1.0 - tcos * tcos)
    tlogit = logit_scale * (tcos * cos_margin - tsin * sin_margin)
    slope = cos_margin + sin_margin * tcos / tsin
    esum = esum + jnp.where(mine, jnp.exp(tlogit - logit_scale), 0.0)
    ssend[0:1] = esum
    ssend[1:2] = jnp.where(mine, tlogit, 0.0)
    srecv[me] = ssend[...]
    send_to(2, lambda dst: ssend, srecv, 1, n)
    wait_all(rsems, 2, srecv, n - 1)
    send_to(1, lambda dst: fsend.at[dst], frecv, half, n)
    stats = jnp.sum(srecv[...], axis=0)
    log_total = logit_scale + jnp.log(stats[0:1])
    loss_out[...] = log_total - stats[1:2]
    tgrad = logit_scale * (jnp.exp(tlogit - log_total) - 1.0) * slope

    def grad_cos(k):
        at = pl.ds(pl.multiple_of(k * rows, rows), rows)
        hit = class_ids == local - k * rows
        probs = jnp.exp(logit_scale * cosines[at] - log_total)
        return jnp.where(hit, tgrad, logit_scale * probs).astype(bf16)

    acc[...] = jnp.zeros_like(acc)

    def embed_grads(k, carry):
        at = pl.ds(pl.multiple_of(k * rows, rows), rows)
        acc[...] += lax.dot_general(
            grad_cos(k), clow[at], (((0,), (0,)), ((), ())), preferred_element_type=f32
        )
        return carry

    lax.fori_loop(0, blocks, embed_grads, 0)
    psend[...] = acc[...].astype(bf16).reshape(n, tok, width)
    send_partner(6, lambda j: psend.at[2 * j + 1 - core], lambda j: pair.at[j])

    def out_copy(k, slot):
        at = pl.ds(pl.multiple_of(k * rows, rows), rows)
        return pltpu.make_async_copy(stage.at[slot], gc_out.at[at], osem.at[slot])

    def center_grads(k, carry):
        at = pl.ds(pl.multiple_of(k * rows, rows), rows)
        unit = jnp.dot(
            grad_cos(k), emb[...].reshape(batch, width), preferred_element_type=f32
        )
        inv = inv_c[at]
        direction = cbuf[at].astype(f32) * inv
        along = jnp.sum(unit * direction, axis=1, keepdims=True)
        slot = lax.rem(k, 2)

        @pl.when(k >= 2)
        def _():
            out_copy(k - 2, slot).wait()

        stage[slot] = ((unit - direction * along) * inv).astype(bf16)
        out_copy(k, slot).start()
        return carry

    lax.fori_loop(0, 1, center_grads, 0)
    wait_all(rsems, 6, pair, half)

    def add_pair(j, carry):
        at = pl.ds(pl.multiple_of((2 * j + core) * tok, tok), tok)
        psend[2 * j + core] = (acc[at] + pair[j].astype(f32)).astype(bf16)
        return carry

    lax.fori_loop(0, half, add_pair, 0)
    precv[chip] = psend[me]
    send_chips(3, lambda to: psend.at[2 * to + core], precv, chip)
    lax.fori_loop(1, blocks, center_grads, 0)

    wait_all(rsems, 3, precv, half - 1)
    grad_dir = jnp.sum(precv[...].astype(f32), axis=0)
    own = esend[...].astype(f32)
    inv_emb = inverse_norm(own)
    emb_dir = own * inv_emb
    along = jnp.sum(grad_dir * emb_dir, axis=1, keepdims=True)
    grad_emb = ((grad_dir - emb_dir * along) * inv_emb).astype(bf16)
    gsend[...] = grad_emb
    grecv[me] = grad_emb
    send_chips(4, lambda to: gsend, grecv, me)

    wait_all(rsems, 1, frecv, n - 1)
    for k in range(max(blocks - 2, 0), blocks):
        out_copy(k, k % 2).wait()
    wait_all(rsems, 4, grecv, half - 1)
    send_partner(7, lambda j: grecv.at[2 * j + core], lambda j: grecv.at[2 * j + core])
    wait_all(rsems, 7, grecv, half)
    fc_out[...] = lax.dot_general(
        frecv[...].reshape(batch, part), grecv[...].reshape(batch, width),
        (((0,), (0,)), ((), ())), preferred_element_type=f32,
    )
    wait_all(ssems, 0, emb, half - 1)
    wait_all(ssems, 1, frecv, n - 1)
    wait_all(ssems, 2, srecv, n - 1)
    wait_all(ssems, 3, precv, half - 1)
    wait_all(ssems, 4, grecv, half - 1)
    wait_all(ssems, 6, pair, half)
    wait_all(ssems, 7, grecv, half)


def on_device(features, fc_weight, centers, labels):
    n = lax.axis_size("cls")
    tok, feats = features.shape
    classes, width = centers.shape
    batch = labels.shape[0]
    rows = min(512, 262144 // batch)
    slots = 4 if batch <= 1024 else 2
    chunk = 128 * largest_divisor(feats // 128, 14)
    part = feats // n
    vmem = pl.BlockSpec(memory_space=pltpu.VMEM)
    hbm = pl.BlockSpec(memory_space=pl.ANY)
    loss_row, grad_centers, grad_fc = pl.pallas_call(
        functools.partial(kernel, n, rows, slots),
        out_shape=(
            jax.ShapeDtypeStruct((1, batch), f32),
            jax.ShapeDtypeStruct((classes, width), bf16),
            jax.ShapeDtypeStruct((part, width), f32),
        ),
        in_specs=[vmem, hbm, hbm, vmem],
        out_specs=(vmem, hbm, vmem),
        scratch_shapes=[
            pltpu.VMEM((slots, chunk, width), bf16),
            pltpu.VMEM((classes, width), bf16),
            pltpu.VMEM((classes, width), bf16),
            pltpu.VMEM((classes, 1), f32),
            pltpu.VMEM((classes, batch), f32),
            pltpu.VMEM((batch, width), f32),
            pltpu.VMEM((tok, width), bf16),
            pltpu.VMEM((n, tok, width), bf16),
            pltpu.VMEM((n, tok, part), bf16),
            pltpu.VMEM((n, tok, part), bf16),
            pltpu.VMEM((2, batch), f32),
            pltpu.VMEM((n, 2, batch), f32),
            pltpu.VMEM((n, tok, width), bf16),
            pltpu.VMEM((n // 2, tok, width), bf16),
            pltpu.VMEM((n // 2, tok, width), bf16),
            pltpu.VMEM((tok, width), bf16),
            pltpu.VMEM((n, tok, width), bf16),
            pltpu.VMEM((2, rows, width), bf16),
            pltpu.SemaphoreType.DMA((slots,)),
            pltpu.SemaphoreType.DMA,
            pltpu.SemaphoreType.DMA((2,)),
            pltpu.SemaphoreType.DMA((8,)),
            pltpu.SemaphoreType.DMA((8,)),
        ],
        compiler_params=pltpu.CompilerParams(
            collective_id=0, has_side_effects=True, vmem_limit_bytes=67043328
        ),
    )(features, fc_weight, centers, labels[None])
    loss = lax.dynamic_slice_in_dim(loss_row[0], lax.axis_index("cls") * tok, tok)
    return (loss, grad_centers, grad_fc)


def solution(mesh):
    placed = (P("cls", None), P(), P("cls", None), P())
    return jax.shard_map(
        on_device,
        mesh=mesh,
        in_specs=placed,
        out_specs=(P("cls"), P("cls", None), P("cls", None)),
        check_vma=False,
    )
```

profile of v0, /device:TPU:0, one launch (start us, length us, event | category | flops | bytes accessed | tf_op | source)
XLA Modules:
  0.0 63.2 jit_solution(2974656370171542139)
XLA Ops:
  0.6 56.0 %shard_map.67 = (f32[1,512]{1,0:T(1,128)}, bf16[4096,512]{1,0:T(8,128)(2,1)}, f32[392,512]{1,0:T(8,128)}) custom-call(bf16[16,12544]{1,0:T(8,128)(2,1)} %feat.1, bf16[12544,512]{1,0:T(8,128)(2,1)} %weight.1, bf16[4096,512]{1,0:T(8,128)(2,1)} %centers_hbm.1, s32[1,512]{1,0:T(1,128)} %bitcast.3), custom_call_target="tpu_custom_call" | custom-call | tf_op jit(solution)/shard_map/pallas_call | solution.py:274
  56.6 1.2 %dynamic-slice_bitcast_fusion = f32[16]{0:T(128)} fusion(f32[1,512]{1,0:T(1,128)} %get-tuple-element.6, s32[]{:T(128)S(6)} %select_n.3), kind=kLoop, calls=%fused_computation | loop fusion | bytes 132 | tf_op jit(solution)/shard_map/dynamic_slice | solution.py:312
  57.8 0.0 copy-start
  57.8 4.5 %copy.9 = bf16[4096,512]{1,0:T(8,128)(2,1)} copy(bf16[4096,512]{1,0:T(8,128)(2,1)} %get-tuple-element.13) | data formatting | bytes 8388608
  62.3 0.0 copy-done
  62.3 0.9 %copy.10 = f32[392,512]{1,0:T(8,128)} copy(f32[392,512]{1,0:T(8,128)S(1)} %copy-done) | data formatting | bytes 1605632
Async XLA Ops:
  57.8 4.5 %copy-start = (f32[392,512]{1,0:T(8,128)S(1)}, f32[392,512]{1,0:T(8,128)}, u32[]{:S(2)}) copy-start(f32[392,512]{1,0:T(8,128)} %get-tuple-element.14) | copy-start | bytes 2408452
where the time goes:
time: 63.7 us; the launch traced here: 63.2 us
  Pallas kernels  56 us (88%)
  local copies, waits for them, and re-layouts  6.61 us (10%)
  between operations  0.65 us (1%)
    pallas_call x1, Pallas kernels, on_device(): pl.pallas_call(functools.partial(kernel, n, rows, slots), out_shape=(jax....  56 us
    unnamed x4, local copies, waits for them, and re-layouts  5.43 us

commit v1 on v0

v1 whole, which is shorter than its diff:
```python
import functools
import math

import jax
import jax.numpy as jnp
from jax import lax
from jax.experimental import pallas as pl
from jax.experimental.pallas import tpu as pltpu
from jax.sharding import PartitionSpec as P

logit_scale = 64.0
cos_margin = math.cos(0.5)
sin_margin = math.sin(0.5)
epsilon = 1e-06
exp2_scale = logit_scale * math.log2(math.e)
lanes = 128
MESH = pl.DeviceIdType.MESH
f32, bf16 = jnp.float32, jnp.bfloat16


def inverse_norm(values):
    return lax.rsqrt(jnp.sum(values * values, axis=1, keepdims=True) + epsilon)


def largest_divisor(number, most):
    return next(d for d in range(most, 0, -1) if number % d == 0)


def repeat(count, body, unroll):
    if unroll:
        for k in range(count):
            body(k)
    else:
        lax.fori_loop(0, count, lambda k, carry: (body(k), carry)[1], 0)


def ds(k, size):
    return pl.ds(k * size if isinstance(k, int) else pl.multiple_of(k * size, size), size)


def row_sums(values):
    part = values[:, :lanes]
    for j in range(1, values.shape[1] // lanes):
        part = part + values[:, j * lanes : (j + 1) * lanes]
    return jnp.sum(part.T, axis=0, keepdims=True)


def column(row):
    return jnp.broadcast_to(row, (lanes, row.shape[1])).T


def main_kernel(
    n, rows, slots, feat_hbm, weight, centers_hbm, labels,
    loss_out, gc_out, features_out, grads_out,
    feat, wbuf, cbuf, clow, inv_c, expo, sums, acc, target, esend, emb, scaled,
    lab, tfix, fsend, ssend, srecv, psend, pair, precv, gsend,
    fsem, wsem, csem, ssems, rsems,
):
    me = lax.axis_index("cls")
    tok, feats = feat.shape
    classes, width = cbuf.shape
    batch = n * tok
    chunk = wbuf.shape[1]
    chunks = feats // chunk
    blocks = classes // rows
    part = feats // n
    half = n // 2
    core = lax.rem(me, 2)
    chip = me // 2
    partner = me + 1 - 2 * core
    side = me // half
    near, far = side * half, (1 - side) * half
    unroll = batch <= 512
    group = min(batch, 512)
    frecv, grecv = features_out, grads_out

    pieces = largest_divisor(chunks, 14)
    piece = feats // pieces

    def feat_copy(c):
        at = pl.ds(c * piece, piece)
        return pltpu.make_async_copy(feat_hbm.at[:, at], feat.at[:, at], fsem)

    def weight_copy(c):
        return pltpu.make_async_copy(
            weight.at[pl.ds(c * chunk, chunk)], wbuf.at[c % slots], wsem.at[c % slots]
        )

    ahead = min(slots, 6)
    for c in range(pieces):
        feat_copy(c).start()
    for c in range(min(ahead, chunks)):
        weight_copy(c).start()
    centers_copy = pltpu.make_async_copy(centers_hbm, cbuf, csem)

    barrier = pltpu.get_barrier_semaphore()

    def greet(i, carry):
        pl.semaphore_signal(barrier, inc=1, device_id=(lax.rem(me + i, n),), device_id_type=MESH)
        return carry

    lax.fori_loop(1, n, greet, 0)

    def send_features(base, first, last):
        def step(i, carry):
            dst = base + lax.rem(me + i, half)
            pltpu.make_async_remote_copy(
                src_ref=fsend.at[dst], dst_ref=frecv.at[me],
                send_sem=ssems.at[1], recv_sem=rsems.at[1],
                device_id=(dst,), device_id_type=MESH,
            ).start()
            return carry

        lax.fori_loop(first, last, step, 0)

    def send_all(phase, source, target):
        def step(i, carry):
            dst = lax.rem(me + i, n)
            pltpu.make_async_remote_copy(
                src_ref=source, dst_ref=target.at[me],
                send_sem=ssems.at[phase], recv_sem=rsems.at[phase],
                device_id=(dst,), device_id_type=MESH,
            ).start()
            return carry

        lax.fori_loop(1, n, step, 0)

    def wait_all(sems, phase, target, count):
        whole = target.at[pl.ds(0, count)]
        pltpu.make_async_copy(whole, whole, sems.at[phase]).wait()

    def send_chips(phase, source, target, slot):
        def step(i, carry):
            to = lax.rem(chip + i, half)
            pltpu.make_async_remote_copy(
                src_ref=source(to), dst_ref=target.at[slot],
                send_sem=ssems.at[phase], recv_sem=rsems.at[phase],
                device_id=(2 * to + core,), device_id_type=MESH,
            ).start()
            return carry

        lax.fori_loop(1, half, step, 0)

    def send_partner(phase, source, target):
        def step(j, carry):
            pltpu.make_async_remote_copy(
                src_ref=source(j), dst_ref=target(j),
                send_sem=ssems.at[phase], recv_sem=rsems.at[phase],
                device_id=(partner,), device_id_type=MESH,
            ).start()
            return carry

        lax.fori_loop(0, half, step, 0)

    pltpu.make_async_copy(feat_hbm, feat, fsem).wait()
    for j in range(n):
        fsend[j] = feat[:, j * part : (j + 1) * part]
    frecv[me] = fsend[me]
    local = labels[...] - me * classes
    lab[...] = column(local.astype(f32)).astype(jnp.int32)
    total = jnp.zeros((tok, width), f32)
    for c in range(chunks):
        if c == min(3, chunks - 1):
            pl.semaphore_wait(barrier, n - 1)
            send_features(far, 0, half // 2)
        weight_copy(c).wait()
        total = total + jnp.dot(
            feat[:, c * chunk : (c + 1) * chunk], wbuf[c % slots], preferred_element_type=f32
        )
        if c + ahead < chunks:
            weight_copy(c + ahead).start()
        if c == max(chunks - ahead, 0):
            centers_copy.start()
    esend[...] = total.astype(bf16)
    emb[me] = total.astype(bf16)
    send_chips(0, lambda to: esend, emb, me)

    centers_copy.wait()

    def normalise(k):
        at = ds(k, rows)
        block = cbuf[at].astype(f32)
        inv = inverse_norm(block)
        inv_c[at] = jnp.broadcast_to(inv, (rows, lanes))
        clow[at] = (block * inv).astype(bf16)

    repeat(blocks, normalise, unroll)

    def hits(g, first):
        ids = lax.broadcasted_iota(jnp.int32, (group, lanes), 1) + first
        return ids == lab[ds(g, group)]

    def find_targets(g):
        def block(k):
            chosen = jnp.concatenate(
                [
                    jnp.where(hits(g, k * rows + j * lanes), 1.0, 0.0).astype(bf16)
                    for j in range(rows // lanes)
                ],
                axis=1,
            )
            acc[ds(g, group)] += jnp.dot(chosen, clow[ds(k, rows)], preferred_element_type=f32)

        acc[ds(g, group)] = jnp.zeros((group, width), f32)
        repeat(blocks, block, unroll)
        target[ds(g, group)] = acc[ds(g, group)].astype(bf16)

    repeat(batch // group, find_targets, unroll)

    wait_all(rsems, 0, emb, half - 1)
    send_partner(5, lambda j: emb.at[2 * j + core], lambda j: emb.at[2 * j + core])
    send_features(far, half // 2, half)
    wait_all(rsems, 5, emb, half)
    wait_all(ssems, 5, emb, half)

    all_emb = emb[...].reshape(batch, width).astype(f32)
    emb_low = (all_emb * inverse_norm(all_emb)).astype(bf16)
    emb[...] = emb_low.reshape(n, tok, width)
    tcos = row_sums(emb_low.astype(f32) * target[...].astype(f32))
    mine = (local >= 0) & (local < classes)
    tsin = jnp.sqrt(1.0 - tcos * tcos)
    tlogit = logit_scale * (tcos * cos_margin - tsin * sin_margin)
    slope = cos_margin + sin_margin * tcos / tsin
    texp = jnp.exp(tlogit)

    def forward(g):
        picked = emb[ds(g, group // tok)].reshape(group, width)
        sums[ds(g, group)] = jnp.zeros((group, lanes), f32)

        def block(k):
            cos = lax.dot_general(
                picked, clow[ds(k, rows)], (((1,), (1,)), ((), ())), preferred_element_type=f32
            )
            row = jnp.zeros((group, lanes), f32)
            for j in range(rows // lanes):
                power = jnp.exp2(exp2_scale * cos[:, j * lanes : (j + 1) * lanes])
                power = jnp.where(hits(g, k * rows + j * lanes), 0.0, power)
                row = row + power
                expo[ds(g, group), ds(k * (rows // lanes) + j, lanes)] = power.astype(bf16)
            sums[ds(g, group)] += row

        repeat(blocks, block, unroll)

    repeat(batch // group, forward, unroll)
    ssend[0:1] = row_sums(sums[...]) + jnp.where(mine, texp, 0.0)
    ssend[1:2] = jnp.where(mine, tlogit, 0.0)
    srecv[me] = ssend[...]
    send_all(2, ssend, srecv)

    def weigh(g):
        acc[ds(g, 256)] = jnp.dot(expo[ds(g, 256)], clow[...], preferred_element_type=f32)

    repeat(batch // 256, weigh, unroll)
    wait_all(rsems, 2, srecv, n - 1)
    stats = jnp.sum(srecv[...], axis=0)
    norm = stats[0:1]
    loss_row = jnp.log(norm) - stats[1:2]
    tgrad = jnp.where(mine, logit_scale * (texp / norm - 1.0) * slope, 0.0)
    scale = column(logit_scale / norm)
    tscale = column(tgrad)
    tfix[...] = column((texp - norm) * slope)

    for j in range(width // lanes):
        at = slice(j * lanes, (j + 1) * lanes)
        total = scale * acc[:, at] + tscale * target[:, at].astype(f32)
        acc[:, at] = total
        psend[:, :, at] = total.astype(bf16).reshape(n, tok, lanes)
    send_partner(6, lambda j: psend.at[2 * j + 1 - core], lambda j: pair.at[j])
    own_row = lax.broadcasted_iota(jnp.int32, (tok, batch), 0) + me * tok
    own_lane = lax.broadcasted_iota(jnp.int32, (tok, batch), 1)
    picked_loss = jnp.where(own_row == own_lane, loss_row, 0.0)
    loss_out[...] = row_sums(picked_loss)
    for j in range(width // lanes):
        at = slice(j * lanes, (j + 1) * lanes)
        low = emb[:, :, at].reshape(batch, lanes).astype(f32)
        scaled[:, at] = (low * scale).astype(bf16)
    wait_all(rsems, 6, pair, half)

    def add_pair(j, carry):
        at = pl.ds(pl.multiple_of((2 * j + core) * tok, tok), tok)
        psend[2 * j + core] = (acc[at] + pair[j].astype(f32)).astype(bf16)
        return carry

    lax.fori_loop(0, half, add_pair, 0)
    precv[chip] = psend[me]
    send_chips(3, lambda to: psend.at[2 * to + core], precv, chip)
    send_features(near, 1, half)

    ones = jnp.ones((width, lanes), bf16)

    def center_grads(k, carry):
        at = ds(k, rows)
        weights = []
        for j in range(rows // lanes):
            block = expo[:, ds(k * (rows // lanes) + j, lanes)].astype(f32)
            ids = lax.broadcasted_iota(jnp.int32, (batch, lanes), 1) + (k * rows + j * lanes)
            weights.append(jnp.where(ids == lab[...], tfix[...], block).astype(bf16))
        unit = lax.dot_general(
            jnp.concatenate(weights, axis=1), scaled[...], (((0,), (0,)), ((), ())),
            preferred_element_type=f32,
        )
        center = cbuf[at].astype(f32)
        along = jnp.dot((unit * center).astype(bf16), ones, preferred_element_type=f32)
        inv = inv_c[at]
        along = along * (inv * inv * inv)
        for j in range(width // lanes):
            cols = slice(j * lanes, (j + 1) * lanes)
            gc_out[at, cols] = (unit[:, cols] * inv - center[:, cols] * along).astype(bf16)
        return carry

    early = 5 * blocks // 8
    lax.fori_loop(0, early, center_grads, 0)

    wait_all(rsems, 3, precv, half - 1)
    grad_dir = jnp.sum(precv[...].astype(f32), axis=0)
    own = esend[...].astype(f32)
    inv_emb = inverse_norm(own)
    emb_dir = own * inv_emb
    along = jnp.sum(grad_dir * emb_dir, axis=1, keepdims=True)
    grad_emb = ((grad_dir - emb_dir * along) * inv_emb).astype(bf16)
    gsend[...] = grad_emb
    grecv[me] = grad_emb
    send_chips(4, lambda to: gsend, grecv, me)
    lax.fori_loop(early, blocks, center_grads, 0)

    wait_all(rsems, 1, frecv, n - 1)
    wait_all(rsems, 4, grecv, half - 1)
    send_partner(7, lambda j: grecv.at[2 * j + core], lambda j: grecv.at[2 * j + core])
    wait_all(ssems, 0, emb, half - 1)
    wait_all(ssems, 1, frecv, n - 1)
    wait_all(ssems, 2, srecv, n - 1)
    wait_all(ssems, 3, precv, half - 1)
    wait_all(ssems, 4, grecv, half - 1)
    wait_all(ssems, 6, pair, half)
    wait_all(rsems, 7, grecv, half)
    wait_all(ssems, 7, grecv, half)


def last_kernel(gc, features, grads, loss, loss_out, gc_out, fc_out, stage, sems):
    gc_copy = pltpu.make_async_copy(gc, gc_out, sems.at[0])
    gc_copy.start()
    n, tok, part = features.shape
    stage[...] = lax.dot_general(
        features[...].reshape(n * tok, part), grads[...].reshape(n * tok, grads.shape[2]),
        (((0,), (0,)), ((), ())), preferred_element_type=f32,
    )
    fc_copy = pltpu.make_async_copy(stage, fc_out, sems.at[1])
    fc_copy.start()
    loss_out[...] = loss[0]
    gc_copy.wait()
    fc_copy.wait()


def on_device(features, fc_weight, centers, labels):
    n = lax.axis_size("cls")
    tok, feats = features.shape
    classes, width = centers.shape
    batch = labels.shape[0]
    rows = 256
    chunk = lanes * largest_divisor(feats // lanes, 7)
    slots = feats // chunk if batch <= 1024 else 2
    part = feats // n
    vmem = pl.BlockSpec(memory_space=pltpu.VMEM)
    hbm = pl.BlockSpec(memory_space=pl.ANY)
    loss, gc, spread, grads = pl.pallas_call(
        functools.partial(main_kernel, n, rows, slots),
        out_shape=(
            pltpu.VMEM((1, tok), f32),
            pltpu.VMEM((classes, width), bf16),
            pltpu.VMEM((n, tok, part), bf16),
            pltpu.VMEM((n, tok, width), bf16),
        ),
        in_specs=[hbm, hbm, hbm, vmem],
        out_specs=(vmem, vmem, vmem, vmem),
        scratch_shapes=[
            pltpu.VMEM((tok, feats), bf16),
            pltpu.VMEM((slots, chunk, width), bf16),
            pltpu.VMEM((classes, width), bf16),
            pltpu.VMEM((classes, width), bf16),
            pltpu.VMEM((classes, lanes), f32),
            pltpu.VMEM((batch, classes), bf16),
            pltpu.VMEM((batch, lanes), f32),
            pltpu.VMEM((batch, width), f32),
            pltpu.VMEM((batch, width), bf16),
            pltpu.VMEM((tok, width), bf16),
            pltpu.VMEM((n, tok, width), bf16),
            pltpu.VMEM((batch, width), bf16),
            pltpu.VMEM((batch, lanes), jnp.int32),
            pltpu.VMEM((batch, lanes), f32),
            pltpu.VMEM((n, tok, part), bf16),
            pltpu.VMEM((2, batch), f32),
            pltpu.VMEM((n, 2, batch), f32),
            pltpu.VMEM((n, tok, width), bf16),
            pltpu.VMEM((n // 2, tok, width), bf16),
            pltpu.VMEM((n // 2, tok, width), bf16),
            pltpu.VMEM((tok, width), bf16),
            pltpu.SemaphoreType.DMA,
            pltpu.SemaphoreType.DMA((slots,)),
            pltpu.SemaphoreType.DMA,
            pltpu.SemaphoreType.DMA((8,)),
            pltpu.SemaphoreType.DMA((8,)),
        ],
        compiler_params=pltpu.CompilerParams(
            collective_id=0, has_side_effects=True, vmem_limit_bytes=54 * 2**20
        ),
    )(features, fc_weight, centers, labels[None])
    return pl.pallas_call(
        last_kernel,
        out_shape=(
            jax.ShapeDtypeStruct((tok,), f32),
            jax.ShapeDtypeStruct((classes, width), bf16),
            jax.ShapeDtypeStruct((part, width), f32),
        ),
        in_specs=[vmem, vmem, vmem, vmem],
        out_specs=(vmem, hbm, hbm),
        scratch_shapes=[pltpu.VMEM((part, width), f32), pltpu.SemaphoreType.DMA((2,))],
        compiler_params=pltpu.CompilerParams(vmem_limit_bytes=8 * 2**20),
    )(gc, spread, grads, loss)


def solution(mesh):
    placed = (P("cls", None), P(), P("cls", None), P())
    return jax.shard_map(
        on_device,
        mesh=mesh,
        in_specs=placed,
        out_specs=(P("cls"), P("cls", None), P("cls", None)),
        check_vma=False,
    )
```

time: 63.7 us -> 53.4 us (0.84)
  local copies, waits for them, and re-layouts: 6.61 us -> 0 us
  Pallas kernels: 56 us -> 52.6 us
    unnamed x4 -> x0, local copies, waits for them, and re-layouts: 5.43 us -> none
    pallas_call x1 -> x2, Pallas kernels: 56 us -> 52.6 us  [the longest x1 49.7 us: on_device(): pl.pallas_call(functools.partial(main_kernel, n, rows, slots), out_shape=...]
    dynamic_slice x1 -> x0, local copies, waits for them, and re-layouts: 1.18 us -> none  [on_device(): lax.dynamic_slice_in_dim(loss_row[0], lax.axis_index('cls') * tok, tok)]
where the time goes in v1:
time: 53.4 us; the launch traced here: 53.2 us
  Pallas kernels  52.6 us (99%)
  between operations  0.64 us (1%)
    pallas_call x1, Pallas kernels, on_device(): pl.pallas_call(functools.partial(main_kernel, n, rows, slots), out_shape=...  49.7 us
    pallas_call x1, Pallas kernels, on_device(): pl.pallas_call(last_kernel, out_shape=(jax.ShapeDtypeStruct((tok,), f32),...  2.9 us

profile of v1, /device:TPU:0, one launch (start us, length us, event | category | flops | bytes accessed | tf_op | source)
XLA Modules:
  0.0 53.2 jit_solution(11996499896436996347)
XLA Ops:
  0.6 49.7 %shard_map.67 = (f32[1,16]{1,0:T(1,128)S(1)}, bf16[4096,512]{1,0:T(8,128)(2,1)S(1)}, bf16[32,16,392]{2,1,0:T(8,128)(2,1)S(1)}, bf16[32,16,512]{2,1,0:T(8,128)(2,1)S(1)}) custom-call(bf16[16,12544]{1,0:T(8,128)(2,1)} %feat_hbm.1, bf16[12544,512]{1,0:T(8,128)(2,1)} %weight.1, bf16[4096,512]{1,0:T(8,128)(2,1)} %centers_hbm.1, s32[1,512]{1,0:T(1,128)} %bitcast.1), custom_call_target="tpu_custom_call" | custom-call | tf_op jit(solution)/shard_map/pallas_call | solution.py:365
  50.3 2.9 %shard_map.68 = (f32[16]{0:T(128)}, bf16[4096,512]{1,0:T(8,128)(2,1)}, f32[392,512]{1,0:T(8,128)}) custom-call(bf16[4096,512]{1,0:T(8,128)(2,1)S(1)} %get-tuple-element.7.gc, bf16[32,16,392]{2,1,0:T(8,128)(2,1)S(1)} %get-tuple-element.8.features, bf16[32,16,512]{2,1,0:T(8,128)(2,1)S(1)} %get-tuple-element.9.grads, f32[1,16]{1,0:T(1,128)S(1)} %get-tuple-element.10.loss), custom_call_target="tpu_custom_call" | custom-call | tf_op jit(solution)/shard_map/pallas_call | solution.py:407

commit v2 on v1

v2 whole, which is shorter than its diff:
```python
import functools
import math

import jax
import jax.numpy as jnp
from jax import lax
from jax.experimental import pallas as pl
from jax.experimental.pallas import tpu as pltpu
from jax.sharding import PartitionSpec as P

logit_scale = 64.0
cos_margin = math.cos(0.5)
sin_margin = math.sin(0.5)
epsilon = 1e-06
exp2_scale = logit_scale * math.log2(math.e)
lanes = 128
MESH = pl.DeviceIdType.MESH
f32, bf16 = jnp.float32, jnp.bfloat16


def inverse_norm(values):
    return lax.rsqrt(jnp.sum(values * values, axis=1, keepdims=True) + epsilon)


def largest_divisor(number, most):
    return next(d for d in range(most, 0, -1) if number % d == 0)


def repeat(count, body, unroll):
    if unroll:
        for k in range(count):
            body(k)
    else:
        lax.fori_loop(0, count, lambda k, carry: (body(k), carry)[1], 0)


def ds(k, size):
    return pl.ds(k * size if isinstance(k, int) else pl.multiple_of(k * size, size), size)


def row_sums(values):
    part = values[:, :lanes]
    for j in range(1, values.shape[1] // lanes):
        part = part + values[:, j * lanes : (j + 1) * lanes]
    return jnp.sum(part.T, axis=0, keepdims=True)


def column(row):
    return jnp.broadcast_to(row, (lanes, row.shape[1])).T


def main_kernel(
    n, rows, slots, split, feat_hbm, weight, centers_hbm, labels,
    loss_out, gc_out, features_out, grads_out,
    feat, wbuf, cbuf, clow, inv_c, expo, sums, acc, target, esend, emb, low,
    lab, tfix, fsend, ssend, srecv, psend, pair, tpair, blocks_u, blocks_t,
    far_u, near_u, far_t, near_t, fold_send, fold_recv, gsend,
    fsem, wsem, csem, ssems, rsems,
):
    me = lax.axis_index("cls")
    tok, feats = feat.shape
    classes, width = cbuf.shape
    batch = n * tok
    chunk = wbuf.shape[1]
    chunks = feats // chunk
    blocks = classes // rows
    part = feats // n
    half = n // 2
    quarter = n // 4
    core = lax.rem(me, 2)
    chip = me // 2
    partner = me + 1 - 2 * core
    mirror = lax.rem(me + half, n)
    side = me // half
    near, far = side * half, (1 - side) * half
    place = chip - side * quarter
    unroll = batch <= 512
    group = min(batch // 2, 512)
    groups = batch // 2 // group
    frecv, grecv = features_out, grads_out

    def feat_copy(c):
        at = pl.ds(c * chunk, chunk)
        return pltpu.make_async_copy(feat_hbm.at[:, at], feat.at[:, at], fsem.at[c])

    def weight_start(c):
        size = chunk // split
        for i in range(split):
            pltpu.make_async_copy(
                weight.at[pl.ds(c * chunk + i * size, size)],
                wbuf.at[c % slots, pl.ds(i * size, size)],
                wsem.at[c % slots],
            ).start()

    def weight_wait(c):
        pltpu.make_async_copy(
            weight.at[pl.ds(c * chunk, chunk)], wbuf.at[c % slots], wsem.at[c % slots]
        ).wait()

    barrier = pltpu.get_barrier_semaphore()

    def greet(i, carry):
        pl.semaphore_signal(barrier, inc=1, device_id=(lax.rem(me + i, n),), device_id_type=MESH)
        return carry

    ahead = 4 if slots == chunks else slots
    feat_copy(0).start()
    weight_start(0)
    lax.fori_loop(1, n, greet, 0)
    for c in range(1, chunks):
        feat_copy(c).start()
        if c < ahead:
            weight_start(c)

    def send(phase, source, target_ref, to):
        pltpu.make_async_remote_copy(
            src_ref=source, dst_ref=target_ref,
            send_sem=ssems.at[phase], recv_sem=rsems.at[phase],
            device_id=(to,), device_id_type=MESH,
        ).start()

    def loop(first, last, body):
        lax.fori_loop(first, last, lambda i, carry: (body(i), carry)[1], 0)

    def wait_all(sems, phase, target_ref, count):
        whole = target_ref.at[pl.ds(0, count)]
        pltpu.make_async_copy(whole, whole, sems.at[phase]).wait()

    def mate(i):
        to = lax.rem(place + i, quarter)
        return to, near + 2 * to + core

    def spread_start(phase, own, whole):
        send(phase, own, whole.at[me], mirror)
        loop(1, quarter, lambda i: send(phase + 1, own, whole.at[me], mate(i)[1]))

    def spread_relay(phase, whole):
        wait_all(rsems, phase, whole, 1)
        block = whole.at[mirror]
        loop(1, quarter, lambda i: send(phase + 2, block, block, mate(i)[1]))

    def spread_near(phase, whole):
        wait_all(rsems, phase + 1, whole, quarter - 1)

        def one(j):
            block = whole.at[near + 2 * j + core]
            send(phase + 3, block, block, partner)

        loop(0, quarter, one)

    def spread_far(phase, whole):
        wait_all(rsems, phase + 2, whole, quarter - 1)

        def one(j):
            block = whole.at[far + 2 * j + core]
            send(phase + 4, block, block, partner)

        loop(0, quarter, one)

    def spread_end(phase, whole):
        for i, count in enumerate((1, quarter - 1, quarter - 1, quarter, quarter)):
            wait_all(ssems, phase + i, whole, count)

    def fold_far(phase, parts, buf):
        def one(i):
            to, device = mate(i)
            send(phase, parts.at[(1 - side) * quarter + to], buf.at[place], device)

        loop(1, quarter, one)
        buf[place] = parts[(1 - side) * quarter + place]

    def fold_near(phase, parts, buf):
        def one(i):
            to, device = mate(i)
            send(phase, parts.at[side * quarter + to], buf.at[place], device)

        loop(1, quarter, one)
        buf[place] = parts[chip]

    def fold_cross(phase, far_buf, which):
        wait_all(rsems, phase, far_buf, quarter - 1)
        fold_send[which] = jnp.sum(far_buf[...].astype(f32), axis=0).astype(bf16)
        send(phase + 2, fold_send.at[which], fold_recv.at[which], mirror)

    def fold_end(phase, near_buf, which):
        wait_all(rsems, phase + 1, near_buf, quarter - 1)
        wait_all(rsems, phase + 2, near_buf, 1)
        for i, count in enumerate((quarter - 1, quarter - 1, 1)):
            wait_all(ssems, phase + i, near_buf, count)
        return jnp.sum(near_buf[...].astype(f32), axis=0) + fold_recv[which].astype(f32)

    total = jnp.zeros((tok, width), f32)
    for c in range(chunks):
        feat_copy(c).wait()
        weight_wait(c)
        if slots == chunks and c + ahead < chunks:
            weight_start(c + ahead)
        total = total + jnp.dot(
            feat[:, c * chunk : (c + 1) * chunk], wbuf[c % slots], preferred_element_type=f32
        )
        if slots < chunks and c + ahead < chunks:
            weight_start(c + ahead)
        if c == max(chunks - ahead, 0):
            for i in range(4):
                at = pl.ds(i * (classes // 4), classes // 4)
                pltpu.make_async_copy(centers_hbm.at[at], cbuf.at[at], csem).start()
    esend[...] = total.astype(bf16)
    emb[me] = total.astype(bf16)
    pl.semaphore_wait(barrier, n - 1)
    spread_start(0, esend, emb)
    for j in range(n):
        fsend[j] = feat[:, j * part : (j + 1) * part]
    frecv[me] = fsend[me]
    local = labels[...] - me * classes
    lab[...] = column(local.astype(f32)).astype(jnp.int32)

    pltpu.make_async_copy(centers_hbm, cbuf, csem).wait()

    def normalise(k):
        at = ds(k, rows)
        block = cbuf[at].astype(f32)
        inv = inverse_norm(block)
        inv_c[at] = jnp.broadcast_to(inv, (rows, lanes))
        clow[at] = (block * inv).astype(bf16)

    repeat(blocks, normalise, unroll)
    spread_relay(0, emb)

    def send_features(base, first, last):
        def one(i):
            dst = base + lax.rem(me + i, half)
            send(20, fsend.at[dst], frecv.at[me], dst)

        loop(first, last, one)

    first_part = 5 * half // 8
    send_features(far, 0, first_part)

    def hits(at, first):
        ids = lax.broadcasted_iota(jnp.int32, (group, lanes), 1) + first
        return ids == lab[at]

    def find_targets(g):
        at = ds(g, group)

        def block(k):
            chosen = [
                jnp.where(hits(at, k * rows + j * lanes), 1.0, 0.0).astype(bf16)
                for j in range(rows // lanes)
            ]
            acc[at] += jnp.dot(
                jnp.concatenate(chosen, axis=1), clow[ds(k, rows)], preferred_element_type=f32
            )

        acc[at] = jnp.zeros((group, width), f32)
        repeat(blocks, block, unroll)
        target[ds(g, group // tok)] = acc[at].astype(bf16).reshape(group // tok, tok, width)

    loop(0, groups, find_targets)
    spread_near(0, emb)
    loop(groups, 2 * groups, find_targets)
    loop(0, half, lambda j: send(7, target.at[2 * j + 1 - core], tpair.at[j], partner))

    def forward(g):
        at = ds(g, group)
        raw = emb[ds(g, group // tok)].reshape(group, width).astype(f32)
        picked = (raw * inverse_norm(raw)).astype(bf16)
        low[at] = picked
        sums[at] = jnp.zeros((group, lanes), f32)

        def block(k):
            cos = lax.dot_general(
                picked, clow[ds(k, rows)], (((1,), (1,)), ((), ())), preferred_element_type=f32
            )
            row = jnp.zeros((group, lanes), f32)
            for j in range(rows // lanes):
                power = jnp.exp2(exp2_scale * cos[:, j * lanes : (j + 1) * lanes])
                power = jnp.where(hits(at, k * rows + j * lanes), 0.0, power)
                row = row + power
                expo[at, ds(k * (rows // lanes) + j, lanes)] = power.astype(bf16)
            sums[at] += row

        repeat(blocks, block, unroll)

    def weigh(g):
        at = ds(g, 256)
        acc[at] = jnp.dot(expo[at], clow[...], preferred_element_type=f32)
        psend[ds(g, 256 // tok)] = acc[at].astype(bf16).reshape(256 // tok, tok, width)

    def each_group(base, size, body):
        count = batch // 2 // size
        if count == 1:
            body(base)
        else:
            loop(0, count, lambda g: body(base * count + g))

    def add_target(j):
        mine = target[2 * j + core].astype(f32)
        blocks_t[j] = (mine + tpair[j].astype(f32)).astype(bf16)

    def send_pair(phase, first):
        def one(j):
            send(phase, psend.at[2 * (first + j) + 1 - core], pair.at[first + j], partner)

        loop(0, quarter, one)

    def add_pair(first):
        def one(j):
            to = first + j
            at = pl.ds(pl.multiple_of((2 * to + core) * tok, tok), tok)
            blocks_u[to] = (acc[at] + pair[to].astype(f32)).astype(bf16)

        loop(0, quarter, one)

    near_chips, far_chips = side * quarter, (1 - side) * quarter
    wait_all(rsems, 3, emb, quarter)
    each_group(side, group, forward)
    wait_all(rsems, 7, tpair, half)
    loop(0, half, add_target)
    fold_far(8, blocks_t, far_t)
    fold_near(9, blocks_t, near_t)
    spread_far(0, emb)
    send_features(far, first_part, half)
    each_group(side, 256, weigh)
    send_pair(21, near_chips)
    wait_all(rsems, 4, emb, quarter)
    each_group(1 - side, group, forward)
    wait_all(rsems, 21, pair, quarter)
    add_pair(near_chips)
    fold_near(13, blocks_u, near_u)
    each_group(1 - side, 256, weigh)
    send_pair(11, far_chips)

    mine = (local >= 0) & (local < classes)
    picked = target[...].reshape(batch, width).astype(f32)
    tcos = row_sums(low[...].astype(f32) * picked)
    tsin = jnp.sqrt(1.0 - tcos * tcos)
    texp = jnp.exp(logit_scale * (tcos * cos_margin - tsin * sin_margin))
    slope = cos_margin + sin_margin * tcos / tsin
    ssend[...] = row_sums(sums[...]) + jnp.where(mine, texp, 0.0)
    srecv[me] = ssend[...]

    def send_stats(i):
        to = lax.rem(me + i, n)
        send(22, ssend, srecv.at[me], to)

    wait_all(rsems, 11, pair, quarter)
    add_pair(far_chips)
    fold_far(12, blocks_u, far_u)
    fold_cross(8, far_t, 0)
    loop(1, n, send_stats)
    own = esend[...].astype(f32)
    inv_emb = inverse_norm(own)
    emb_dir = own * inv_emb
    fold_cross(12, far_u, 1)

    wait_all(rsems, 22, srecv, n - 1)
    norm = jnp.sum(srecv[...], axis=0)
    scale = column(logit_scale / norm)
    tfix[...] = column((texp - norm) * slope)
    for j in range(width // lanes):
        at = slice(j * lanes, (j + 1) * lanes)
        low[:, at] = (low[:, at].astype(f32) * scale).astype(bf16)

    ones = jnp.ones((width, lanes), bf16)

    def center_grads(k):
        at = ds(k, rows)
        weights = []
        for j in range(rows // lanes):
            block = expo[:, ds(k * (rows // lanes) + j, lanes)].astype(f32)
            ids = lax.broadcasted_iota(jnp.int32, (batch, lanes), 1) + (k * rows + j * lanes)
            weights.append(jnp.where(ids == lab[...], tfix[...], block).astype(bf16))
        unit = lax.dot_general(
            jnp.concatenate(weights, axis=1), low[...], (((0,), (0,)), ((), ())),
            preferred_element_type=f32,
        )
        center = cbuf[at].astype(f32)
        along = jnp.dot((unit * center).astype(bf16), ones, preferred_element_type=f32)
        inv = inv_c[at]
        along = along * (inv * inv * inv)
        for j in range(width // lanes):
            cols = slice(j * lanes, (j + 1) * lanes)
            gc_out[at, cols] = (unit[:, cols] * inv - center[:, cols] * along).astype(bf16)

    stops = [blocks * i // 16 for i in (0, 3, 8, 13, 16)]
    loop(stops[0], stops[1], center_grads)
    own_target = fold_end(8, near_t, 0)
    own_low = emb_dir.astype(bf16).astype(f32)
    own_cos = jnp.sum(own_low * own_target, axis=1, keepdims=True)
    own_sin = jnp.sqrt(1.0 - own_cos * own_cos)
    own_logit = logit_scale * (own_cos * cos_margin - own_sin * sin_margin)
    own_slope = cos_margin + sin_margin * own_cos / own_sin
    own_row = lax.broadcasted_iota(jnp.int32, (tok, batch), 0) + me * tok
    own_lane = lax.broadcasted_iota(jnp.int32, (tok, batch), 1)
    own_norm = jnp.sum(jnp.where(own_row == own_lane, norm, 0.0), axis=1, keepdims=True)
    loss = jnp.log(own_norm) - own_logit
    loss_out[...] = jnp.broadcast_to(loss, (tok, lanes)).T[0:1]
    own_scale = logit_scale / own_norm
    own_grad = logit_scale * (jnp.exp(own_logit) / own_norm - 1.0) * own_slope
    grad_dir = own_scale * fold_end(12, near_u, 1) + own_grad * own_target
    along = jnp.sum(grad_dir * emb_dir, axis=1, keepdims=True)
    grad_emb = ((grad_dir - emb_dir * along) * inv_emb).astype(bf16)
    gsend[...] = grad_emb
    grecv[me] = grad_emb
    spread_start(15, gsend, grecv)
    loop(stops[1], stops[2], center_grads)
    spread_relay(15, grecv)
    send_features(near, 1, half)
    loop(stops[2], stops[3], center_grads)
    spread_near(15, grecv)
    loop(stops[3], stops[4], center_grads)
    spread_far(15, grecv)
    wait_all(rsems, 20, frecv, n - 1)
    wait_all(ssems, 20, frecv, n - 1)
    wait_all(ssems, 22, srecv, n - 1)
    wait_all(ssems, 7, tpair, half)
    wait_all(ssems, 11, pair, quarter)
    wait_all(ssems, 21, pair, quarter)
    spread_end(0, emb)
    wait_all(rsems, 18, grecv, quarter)
    wait_all(rsems, 19, grecv, quarter)
    spread_end(15, grecv)


def last_kernel(gc, features, grads, loss, loss_out, gc_out, fc_out, stage, sems):
    classes = gc.shape[0]
    pieces = 16
    for i in range(pieces):
        at = pl.ds(i * (classes // pieces), classes // pieces)
        pltpu.make_async_copy(gc.at[at], gc_out.at[at], sems.at[0]).start()
    n, tok, part = features.shape
    stage[...] = lax.dot_general(
        features[...].reshape(n * tok, part), grads[...].reshape(n * tok, grads.shape[2]),
        (((0,), (0,)), ((), ())), preferred_element_type=f32,
    )
    fc_copy = pltpu.make_async_copy(stage, fc_out, sems.at[1])
    fc_copy.start()
    loss_out[...] = loss[0]
    pltpu.make_async_copy(gc, gc_out, sems.at[0]).wait()
    fc_copy.wait()


def on_device(features, fc_weight, centers, labels):
    n = lax.axis_size("cls")
    tok, feats = features.shape
    classes, width = centers.shape
    batch = labels.shape[0]
    rows = 256
    chunk = lanes * largest_divisor(feats // lanes, 14)
    split = largest_divisor(chunk // lanes, 7)
    slots = feats // chunk if batch <= 1024 else 2
    part = feats // n
    vmem = pl.BlockSpec(memory_space=pltpu.VMEM)
    hbm = pl.BlockSpec(memory_space=pl.ANY)
    loss, gc, spread, grads = pl.pallas_call(
        functools.partial(main_kernel, n, rows, slots, split),
        out_shape=(
            pltpu.VMEM((1, tok), f32),
            pltpu.VMEM((classes, width), bf16),
            pltpu.VMEM((n, tok, part), bf16),
            pltpu.VMEM((n, tok, width), bf16),
        ),
        in_specs=[hbm, hbm, hbm, vmem],
        out_specs=(vmem, vmem, vmem, vmem),
        scratch_shapes=[
            pltpu.VMEM((tok, feats), bf16),
            pltpu.VMEM((slots, chunk, width), bf16),
            pltpu.VMEM((classes, width), bf16),
            pltpu.VMEM((classes, width), bf16),
            pltpu.VMEM((classes, lanes), f32),
            pltpu.VMEM((batch, classes), bf16),
            pltpu.VMEM((batch, lanes), f32),
            pltpu.VMEM((batch, width), f32),
            pltpu.VMEM((n, tok, width), bf16),
            pltpu.VMEM((tok, width), bf16),
            pltpu.VMEM((n, tok, width), bf16),
            pltpu.VMEM((batch, width), bf16),
            pltpu.VMEM((batch, lanes), jnp.int32),
            pltpu.VMEM((batch, lanes), f32),
            pltpu.VMEM((n, tok, part), bf16),
            pltpu.VMEM((1, batch), f32),
            pltpu.VMEM((n, 1, batch), f32),
            pltpu.VMEM((n, tok, width), bf16),
            pltpu.VMEM((n // 2, tok, width), bf16),
            pltpu.VMEM((n // 2, tok, width), bf16),
            pltpu.VMEM((n // 2, tok, width), bf16),
            pltpu.VMEM((n // 2, tok, width), bf16),
            pltpu.VMEM((n // 4, tok, width), bf16),
            pltpu.VMEM((n // 4, tok, width), bf16),
            pltpu.VMEM((n // 4, tok, width), bf16),
            pltpu.VMEM((n // 4, tok, width), bf16),
            pltpu.VMEM((2, tok, width), bf16),
            pltpu.VMEM((2, tok, width), bf16),
            pltpu.VMEM((tok, width), bf16),
            pltpu.SemaphoreType.DMA((feats // chunk,)),
            pltpu.SemaphoreType.DMA((slots,)),
            pltpu.SemaphoreType.DMA,
            pltpu.SemaphoreType.DMA((23,)),
            pltpu.SemaphoreType.DMA((23,)),
        ],
        compiler_params=pltpu.CompilerParams(
            collective_id=0, has_side_effects=True, vmem_limit_bytes=57 * 2**20
        ),
    )(features, fc_weight, centers, labels[None])
    return pl.pallas_call(
        last_kernel,
        out_shape=(
            jax.ShapeDtypeStruct((tok,), f32),
            jax.ShapeDtypeStruct((classes, width), bf16),
            jax.ShapeDtypeStruct((part, width), f32),
        ),
        in_specs=[vmem, vmem, vmem, vmem],
        out_specs=(vmem, hbm, hbm),
        scratch_shapes=[pltpu.VMEM((part, width), f32), pltpu.SemaphoreType.DMA((2,))],
        compiler_params=pltpu.CompilerParams(vmem_limit_bytes=8 * 2**20),
    )(gc, spread, grads, loss)


def solution(mesh):
    placed = (P("cls", None), P(), P("cls", None), P())
    return jax.shard_map(
        on_device,
        mesh=mesh,
        in_specs=placed,
        out_specs=(P("cls"), P("cls", None), P("cls", None)),
        check_vma=False,
    )
```

time: 53.4 us -> 44.9 us (0.84)
  Pallas kernels: 52.6 us -> 44.1 us
    pallas_call x1, Pallas kernels: 49.7 us -> 41.2 us  [on_device(): pl.pallas_call(functools.partial(main_kernel, n, rows, slots, split), out...]
where the time goes in v2:
time: 44.9 us; the launch traced here: 44.8 us
  Pallas kernels  44.1 us (98%)
  between operations  0.64 us (1%)
    pallas_call x1, Pallas kernels, on_device(): pl.pallas_call(functools.partial(main_kernel, n, rows, slots, split), out...  41.2 us
    pallas_call x1, Pallas kernels, on_device(): pl.pallas_call(last_kernel, out_shape=(jax.ShapeDtypeStruct((tok,), f32),...  2.9 us

profile of v2, /device:TPU:0, one launch (start us, length us, event | category | flops | bytes accessed | tf_op | source)
XLA Modules:
  0.0 44.8 jit_solution(7598551077264931863)
XLA Ops:
  0.6 41.2 %shard_map.67 = (f32[1,16]{1,0:T(1,128)S(1)}, bf16[4096,512]{1,0:T(8,128)(2,1)S(1)}, bf16[32,16,392]{2,1,0:T(8,128)(2,1)S(1)}, bf16[32,16,512]{2,1,0:T(8,128)(2,1)S(1)}) custom-call(bf16[16,12544]{1,0:T(8,128)(2,1)} %feat_hbm.1, bf16[12544,512]{1,0:T(8,128)(2,1)} %weight.1, bf16[4096,512]{1,0:T(8,128)(2,1)} %centers_hbm.1, s32[1,512]{1,0:T(1,128)} %bitcast.1), custom_call_target="tpu_custom_call" | custom-call | tf_op jit(solution)/shard_map/pallas_call | solution.py:456
  41.9 2.9 %shard_map.68 = (f32[16]{0:T(128)}, bf16[4096,512]{1,0:T(8,128)(2,1)}, f32[392,512]{1,0:T(8,128)}) custom-call(bf16[4096,512]{1,0:T(8,128)(2,1)S(1)} %get-tuple-element.7.gc, bf16[32,16,392]{2,1,0:T(8,128)(2,1)S(1)} %get-tuple-element.8.features, bf16[32,16,512]{2,1,0:T(8,128)(2,1)S(1)} %get-tuple-element.9.grads, f32[1,16]{1,0:T(1,128)S(1)} %get-tuple-element.10.loss), custom_call_target="tpu_custom_call" | custom-call | tf_op jit(solution)/shard_map/pallas_call | solution.py:506

commit v3 on v2

--- a/solution.py
+++ b/solution.py
@@ -54,7 +54,7 @@
     loss_out, gc_out, features_out, grads_out,
     feat, wbuf, cbuf, clow, inv_c, expo, sums, acc, target, esend, emb, low,
     lab, tfix, fsend, ssend, srecv, psend, pair, tpair, blocks_u, blocks_t,
-    far_u, near_u, far_t, near_t, fold_send, fold_recv, gsend,
+    far_u, across_u, near_u, far_t, near_t, fold_send, fold_recv, gsend,
     fsem, wsem, csem, ssems, rsems,
 ):
     me = lax.axis_index("cls")
@@ -74,6 +74,9 @@
     side = me // half
     near, far = side * half, (1 - side) * half
     place = chip - side * quarter
+    eighth = n // 8
+    plane = place // eighth
+    spot = place - plane * eighth
     unroll = batch <= 512
     group = min(batch // 2, 512)
     groups = batch // 2 // group
@@ -130,14 +133,27 @@
         to = lax.rem(place + i, quarter)
         return to, near + 2 * to + core
 
-    def spread_start(phase, own, whole):
+    def plane_mate(i):
+        to = plane * eighth + lax.rem(spot + i, eighth)
+        return to, near + 2 * to + core
+
+    def across(i):
+        to = (1 - plane) * eighth + lax.rem(spot + i, eighth)
+        return to, far + 2 * to + core
+
+    def spread_mirror(phase, own, whole):
         send(phase, own, whole.at[me], mirror)
+
+    def spread_half(phase, own, whole):
         loop(1, quarter, lambda i: send(phase + 1, own, whole.at[me], mate(i)[1]))
+
+    def spread_across(direct, own, whole):
+        loop(0, eighth, lambda i: send(direct, own, whole.at[me], across(i)[1]))
 
     def spread_relay(phase, whole):
         wait_all(rsems, phase, whole, 1)
         block = whole.at[mirror]
-        loop(1, quarter, lambda i: send(phase + 2, block, block, mate(i)[1]))
+        loop(1, eighth, lambda i: send(phase + 2, block, block, plane_mate(i)[1]))
 
     def spread_near(phase, whole):
         wait_all(rsems, phase + 1, whole, quarter - 1)
@@ -148,8 +164,9 @@
 
         loop(0, quarter, one)
 
-    def spread_far(phase, whole):
-        wait_all(rsems, phase + 2, whole, quarter - 1)
+    def spread_far(phase, direct, whole):
+        wait_all(rsems, phase + 2, whole, eighth - 1)
+        wait_all(rsems, direct, whole, eighth)
 
         def one(j):
             block = whole.at[far + 2 * j + core]
@@ -157,9 +174,10 @@
 
         loop(0, quarter, one)
 
-    def spread_end(phase, whole):
-        for i, count in enumerate((1, quarter - 1, quarter - 1, quarter, quarter)):
+    def spread_end(phase, direct, whole):
+        for i, count in enumerate((1, quarter - 1, eighth - 1, quarter, quarter)):
             wait_all(ssems, phase + i, whole, count)
+        wait_all(ssems, direct, whole, eighth)
 
     def fold_far(phase, parts, buf):
         def one(i):
@@ -169,6 +187,19 @@
         loop(1, quarter, one)
         buf[place] = parts[(1 - side) * quarter + place]
 
+    def fold_plane(phase, direct, parts, buf, direct_buf):
+        def one(i):
+            to, device = plane_mate(i)
+            send(phase, parts.at[(1 - side) * quarter + to], buf.at[spot], device)
+
+        def other(i):
+            to, device = across(i)
+            send(direct, parts.at[(1 - side) * quarter + to], direct_buf.at[spot], device)
+
+        loop(1, eighth, one)
+        loop(0, eighth, other)
+        buf[spot] = parts[(1 - side) * quarter + place]
+
     def fold_near(phase, parts, buf):
         def one(i):
             to, device = mate(i)
@@ -177,16 +208,16 @@
         loop(1, quarter, one)
         buf[place] = parts[chip]
 
-    def fold_cross(phase, far_buf, which):
-        wait_all(rsems, phase, far_buf, quarter - 1)
+    def fold_cross(phase, far_buf, which, count):
+        wait_all(rsems, phase, far_buf, count - 1)
         fold_send[which] = jnp.sum(far_buf[...].astype(f32), axis=0).astype(bf16)
         send(phase + 2, fold_send.at[which], fold_recv.at[which], mirror)
 
-    def fold_end(phase, near_buf, which):
+    def fold_end(phase, near_buf, which, count):
         wait_all(rsems, phase + 1, near_buf, quarter - 1)
         wait_all(rsems, phase + 2, near_buf, 1)
-        for i, count in enumerate((quarter - 1, quarter - 1, 1)):
-            wait_all(ssems, phase + i, near_buf, count)
+        for i, sent in enumerate((count - 1, quarter - 1, 1)):
+            wait_all(ssems, phase + i, near_buf, sent)
         return jnp.sum(near_buf[...].astype(f32), axis=0) + fold_recv[which].astype(f32)
 
     total = jnp.zeros((tok, width), f32)
@@ -207,7 +238,9 @@
     esend[...] = total.astype(bf16)
     emb[me] = total.astype(bf16)
     pl.semaphore_wait(barrier, n - 1)
-    spread_start(0, esend, emb)
+    spread_mirror(0, esend, emb)
+    spread_half(0, esend, emb)
+    spread_across(23, esend, emb)
     for j in range(n):
         fsend[j] = feat[:, j * part : (j + 1) * part]
     frecv[me] = fsend[me]
@@ -233,7 +266,7 @@
 
         loop(first, last, one)
 
-    first_part = 5 * half // 8
+    first_part, second_part = 10 * half // 16, 13 * half // 16
     send_features(far, 0, first_part)
 
     def hits(at, first):
@@ -315,21 +348,15 @@
     near_chips, far_chips = side * quarter, (1 - side) * quarter
     wait_all(rsems, 3, emb, quarter)
     each_group(side, group, forward)
+    spread_far(0, 23, emb)
     wait_all(rsems, 7, tpair, half)
     loop(0, half, add_target)
     fold_far(8, blocks_t, far_t)
     fold_near(9, blocks_t, near_t)
-    spread_far(0, emb)
-    send_features(far, first_part, half)
     each_group(side, 256, weigh)
     send_pair(21, near_chips)
     wait_all(rsems, 4, emb, quarter)
     each_group(1 - side, group, forward)
-    wait_all(rsems, 21, pair, quarter)
-    add_pair(near_chips)
-    fold_near(13, blocks_u, near_u)
-    each_group(1 - side, 256, weigh)
-    send_pair(11, far_chips)
 
     mine = (local >= 0) & (local < classes)
     picked = target[...].reshape(batch, width).astype(f32)
@@ -344,15 +371,22 @@
         to = lax.rem(me + i, n)
         send(22, ssend, srecv.at[me], to)
 
+    loop(1, n, send_stats)
+    each_group(1 - side, 256, weigh)
+    send_pair(11, far_chips)
+    wait_all(rsems, 21, pair, quarter)
+    add_pair(near_chips)
+    fold_cross(8, far_t, 0, quarter)
     wait_all(rsems, 11, pair, quarter)
     add_pair(far_chips)
-    fold_far(12, blocks_u, far_u)
-    fold_cross(8, far_t, 0)
-    loop(1, n, send_stats)
+    fold_plane(12, 25, blocks_u, far_u, across_u)
+    fold_near(13, blocks_u, near_u)
     own = esend[...].astype(f32)
     inv_emb = inverse_norm(own)
     emb_dir = own * inv_emb
-    fold_cross(12, far_u, 1)
+    fold_cross(12, far_u, 1, eighth)
+    send_features(far, first_part, second_part)
+    send_features(near, 1, half)
 
     wait_all(rsems, 22, srecv, n - 1)
     norm = jnp.sum(srecv[...], axis=0)
@@ -383,9 +417,15 @@
             cols = slice(j * lanes, (j + 1) * lanes)
             gc_out[at, cols] = (unit[:, cols] * inv - center[:, cols] * along).astype(bf16)
 
-    stops = [blocks * i // 16 for i in (0, 3, 8, 13, 16)]
-    loop(stops[0], stops[1], center_grads)
-    own_target = fold_end(8, near_t, 0)
+    def grads_between(first, last):
+        def two(k):
+            center_grads(2 * k)
+            center_grads(2 * k + 1)
+
+        loop(blocks // 2 * first // 8, blocks // 2 * last // 8, two)
+
+    grads_between(0, 2)
+    own_target = fold_end(8, near_t, 0, quarter)
     own_low = emb_dir.astype(bf16).astype(f32)
     own_cos = jnp.sum(own_low * own_target, axis=1, keepdims=True)
     own_sin = jnp.sqrt(1.0 - own_cos * own_cos)
@@ -398,29 +438,35 @@
     loss_out[...] = jnp.broadcast_to(loss, (tok, lanes)).T[0:1]
     own_scale = logit_scale / own_norm
     own_grad = logit_scale * (jnp.exp(own_logit) / own_norm - 1.0) * own_slope
-    grad_dir = own_scale * fold_end(12, near_u, 1) + own_grad * own_target
+    total = fold_end(12, near_u, 1, eighth)
+    wait_all(rsems, 25, across_u, eighth)
+    total = total + jnp.sum(across_u[...].astype(f32), axis=0)
+    grad_dir = own_scale * total + own_grad * own_target
     along = jnp.sum(grad_dir * emb_dir, axis=1, keepdims=True)
     grad_emb = ((grad_dir - emb_dir * along) * inv_emb).astype(bf16)
     gsend[...] = grad_emb
     grecv[me] = grad_emb
-    spread_start(15, gsend, grecv)
-    loop(stops[1], stops[2], center_grads)
+    spread_mirror(15, gsend, grecv)
+    spread_across(24, gsend, grecv)
+    spread_half(15, gsend, grecv)
+    grads_between(2, 5)
     spread_relay(15, grecv)
-    send_features(near, 1, half)
-    loop(stops[2], stops[3], center_grads)
+    send_features(far, second_part, half)
+    grads_between(5, 7)
     spread_near(15, grecv)
-    loop(stops[3], stops[4], center_grads)
-    spread_far(15, grecv)
+    spread_far(15, 24, grecv)
+    grads_between(7, 8)
     wait_all(rsems, 20, frecv, n - 1)
     wait_all(ssems, 20, frecv, n - 1)
     wait_all(ssems, 22, srecv, n - 1)
     wait_all(ssems, 7, tpair, half)
     wait_all(ssems, 11, pair, quarter)
     wait_all(ssems, 21, pair, quarter)
-    spread_end(0, emb)
+    wait_all(ssems, 25, across_u, eighth)
+    spread_end(0, 23, emb)
     wait_all(rsems, 18, grecv, quarter)
     wait_all(rsems, 19, grecv, quarter)
-    spread_end(15, grecv)
+    spread_end(15, 24, grecv)
 
 
 def last_kernel(gc, features, grads, loss, loss_out, gc_out, fc_out, stage, sems):
@@ -486,7 +532,8 @@
             pltpu.VMEM((n // 2, tok, width), bf16),
             pltpu.VMEM((n // 2, tok, width), bf16),
             pltpu.VMEM((n // 2, tok, width), bf16),
-            pltpu.VMEM((n // 4, tok, width), bf16),
+            pltpu.VMEM((n // 8, tok, width), bf16),
+            pltpu.VMEM((n // 8, tok, width), bf16),
             pltpu.VMEM((n // 4, tok, width), bf16),
             pltpu.VMEM((n // 4, tok, width), bf16),
             pltpu.VMEM((n // 4, tok, width), bf16),
@@ -496,8 +543,8 @@
             pltpu.SemaphoreType.DMA((feats // chunk,)),
             pltpu.SemaphoreType.DMA((slots,)),
             pltpu.SemaphoreType.DMA,
-            pltpu.SemaphoreType.DMA((23,)),
-            pltpu.SemaphoreType.DMA((23,)),
+            pltpu.SemaphoreType.DMA((26,)),
+            pltpu.SemaphoreType.DMA((26,)),
         ],
         compiler_params=pltpu.CompilerParams(
             collective_id=0, has_side_effects=True, vmem_limit_bytes=57 * 2**20

time: 44.9 us -> 43 us (0.958)
  Pallas kernels: 44.1 us -> 42.2 us
    pallas_call x1, Pallas kernels: 41.2 us -> 39.3 us  [on_device(): pl.pallas_call(functools.partial(main_kernel, n, rows, slots, split), out...]
where the time goes in v3:
time: 43 us; the launch traced here: 42.9 us
  Pallas kernels  42.2 us (98%)
  between operations  0.64 us (1%)
    pallas_call x1, Pallas kernels, on_device(): pl.pallas_call(functools.partial(main_kernel, n, rows, slots, split), out...  39.3 us
    pallas_call x1, Pallas kernels, on_device(): pl.pallas_call(last_kernel, out_shape=(jax.ShapeDtypeStruct((tok,), f32),...  2.9 us

profile of v3, /device:TPU:0, one launch (start us, length us, event | category | flops | bytes accessed | tf_op | source)
XLA Modules:
  0.0 42.9 jit_solution(11516789396536258385)
XLA Ops:
  0.6 39.3 %shard_map.67 = (f32[1,16]{1,0:T(1,128)S(1)}, bf16[4096,512]{1,0:T(8,128)(2,1)S(1)}, bf16[32,16,392]{2,1,0:T(8,128)(2,1)S(1)}, bf16[32,16,512]{2,1,0:T(8,128)(2,1)S(1)}) custom-call(bf16[16,12544]{1,0:T(8,128)(2,1)} %feat_hbm.1, bf16[12544,512]{1,0:T(8,128)(2,1)} %weight.1, bf16[4096,512]{1,0:T(8,128)(2,1)} %centers_hbm.1, s32[1,512]{1,0:T(1,128)} %bitcast.1), custom_call_target="tpu_custom_call" | custom-call | tf_op jit(solution)/shard_map/pallas_call | solution.py:502
  40.0 2.9 %shard_map.68 = (f32[16]{0:T(128)}, bf16[4096,512]{1,0:T(8,128)(2,1)}, f32[392,512]{1,0:T(8,128)}) custom-call(bf16[4096,512]{1,0:T(8,128)(2,1)S(1)} %get-tuple-element.7.gc, bf16[32,16,392]{2,1,0:T(8,128)(2,1)S(1)} %get-tuple-element.8.features, bf16[32,16,512]{2,1,0:T(8,128)(2,1)S(1)} %get-tuple-element.9.grads, f32[1,16]{1,0:T(1,128)S(1)} %get-tuple-element.10.loss), custom_call_target="tpu_custom_call" | custom-call | tf_op jit(solution)/shard_map/pallas_call | solution.py:553

commit v4 on v3

--- a/solution.py
+++ b/solution.py
@@ -266,7 +266,7 @@
 
         loop(first, last, one)
 
-    first_part, second_part = 10 * half // 16, 13 * half // 16
+    first_part = 14 * half // 16
     send_features(far, 0, first_part)
 
     def hits(at, first):
@@ -357,6 +357,8 @@
     send_pair(21, near_chips)
     wait_all(rsems, 4, emb, quarter)
     each_group(1 - side, group, forward)
+    each_group(1 - side, 256, weigh)
+    send_pair(11, far_chips)
 
     mine = (local >= 0) & (local < classes)
     picked = target[...].reshape(batch, width).astype(f32)
@@ -372,8 +374,6 @@
         send(22, ssend, srecv.at[me], to)
 
     loop(1, n, send_stats)
-    each_group(1 - side, 256, weigh)
-    send_pair(11, far_chips)
     wait_all(rsems, 21, pair, quarter)
     add_pair(near_chips)
     fold_cross(8, far_t, 0, quarter)
@@ -385,7 +385,7 @@
     inv_emb = inverse_norm(own)
     emb_dir = own * inv_emb
     fold_cross(12, far_u, 1, eighth)
-    send_features(far, first_part, second_part)
+    send_features(far, first_part, half)
     send_features(near, 1, half)
 
     wait_all(rsems, 22, srecv, n - 1)
@@ -424,7 +424,7 @@
 
         loop(blocks // 2 * first // 8, blocks // 2 * last // 8, two)
 
-    grads_between(0, 2)
+    grads_between(0, 1)
     own_target = fold_end(8, near_t, 0, quarter)
     own_low = emb_dir.astype(bf16).astype(f32)
     own_cos = jnp.sum(own_low * own_target, axis=1, keepdims=True)
@@ -449,10 +449,9 @@
     spread_mirror(15, gsend, grecv)
     spread_across(24, gsend, grecv)
     spread_half(15, gsend, grecv)
-    grads_between(2, 5)
+    grads_between(1, 4)
     spread_relay(15, grecv)
-    send_features(far, second_part, half)
-    grads_between(5, 7)
+    grads_between(4, 7)
     spread_near(15, grecv)
     spread_far(15, 24, grecv)
     grads_between(7, 8)

time: 43 us -> 43.3 us (level)
  no operation moved by 1% of the time
where the time goes in v4:
time: 43.3 us; the launch traced here: 43.2 us
  Pallas kernels  42.5 us (98%)
  between operations  0.64 us (1%)
    pallas_call x1, Pallas kernels, on_device(): pl.pallas_call(functools.partial(main_kernel, n, rows, slots, split), out...  39.6 us
    pallas_call x1, Pallas kernels, on_device(): pl.pallas_call(last_kernel, out_shape=(jax.ShapeDtypeStruct((tok,), f32),...  2.9 us

profile of v4, /device:TPU:0, one launch (start us, length us, event | category | flops | bytes accessed | tf_op | source)
XLA Modules:
  0.0 43.2 jit_solution(15162900061103832561)
XLA Ops:
  0.6 39.6 %shard_map.67 = (f32[1,16]{1,0:T(1,128)S(1)}, bf16[4096,512]{1,0:T(8,128)(2,1)S(1)}, bf16[32,16,392]{2,1,0:T(8,128)(2,1)S(1)}, bf16[32,16,512]{2,1,0:T(8,128)(2,1)S(1)}) custom-call(bf16[16,12544]{1,0:T(8,128)(2,1)} %feat_hbm.1, bf16[12544,512]{1,0:T(8,128)(2,1)} %weight.1, bf16[4096,512]{1,0:T(8,128)(2,1)} %centers_hbm.1, s32[1,512]{1,0:T(1,128)} %bitcast.1), custom_call_target="tpu_custom_call" | custom-call | tf_op jit(solution)/shard_map/pallas_call | solution.py:501
  40.3 2.9 %shard_map.68 = (f32[16]{0:T(128)}, bf16[4096,512]{1,0:T(8,128)(2,1)}, f32[392,512]{1,0:T(8,128)}) custom-call(bf16[4096,512]{1,0:T(8,128)(2,1)S(1)} %get-tuple-element.7.gc, bf16[32,16,392]{2,1,0:T(8,128)(2,1)S(1)} %get-tuple-element.8.features, bf16[32,16,512]{2,1,0:T(8,128)(2,1)S(1)} %get-tuple-element.9.grads, f32[1,16]{1,0:T(1,128)S(1)} %get-tuple-element.10.loss), custom_call_target="tpu_custom_call" | custom-call | tf_op jit(solution)/shard_map/pallas_call | solution.py:552
